TPU v7x, 32 devices: a whole 2x2x4 slice. The times are simulated.
32 devices in a mesh: dp: 8 (over z, x), expert: 4 (over y, core).
Axes of the slice: x: 2, y: 2, z: 4, core: 2. Of those that a mesh axis runs over, the one named last changes fastest.
Arguments:
- tokens: bfloat16 [4096, 4096], P(('dp', 'expert')), may hold values from -6 to 6
- grad_out: bfloat16 [4096, 4096], P(('dp', 'expert')), may hold values from -6 to 6
- experts: int32 [4096, 2], P(('dp', 'expert')), may hold values from 0 to 7, all different within a row; in each aligned block of 128 rows (0 to 127, 128 to 255, ...) at most 64 rows name the same one
- gates: bfloat16 [4096, 2], P(('dp', 'expert')), may hold values from 0 to 1, as said below
- router_weight: bfloat16 [8, 4096], replicated, may hold values from -3 to 3
- saved_outputs: bfloat16 [16384, 4096], P(('dp', 'expert')), may hold values from -0.19921875 to 0.19921875
Outputs:
- input_grad: bfloat16 [4096, 4096], P(('dp', 'expert'))
- router_grad: float32 [8, 4096], replicated
- expert_grad: bfloat16 [16384, 4096], P(('dp', 'expert'))
Inputs may be any that keep to these rules, and one draw needn't show every extreme that they name: Within each aligned block of 128 tokens (the tokens of one device), no expert is named by more than 64 slots, and in some blocks an expert is named by exactly 64 slots. The two experts of a token differ. The two gates of a token are positive and add up to one, up to rounding to bfloat16.
All inputs are finite; a program needn't handle non-finite values.
Results may differ from a plain program's by a relative error of at most 0.0085.
Values may be sent and summed in bfloat16 or wider, within the bound.
A program may use at most 64 MiB of HBM per device.

v0:
```python
import jax
import jax.numpy as jnp
from jax import lax
from jax.sharding import PartitionSpec as P


def slot_positions(experts, count):
    slot_expert = experts.reshape(-1)
    onehot = (slot_expert[:, None] == jnp.arange(count, dtype=jnp.int32)[None, :]).astype(jnp.int32)
    before = jnp.cumsum(onehot, axis=0) - onehot
    return (slot_expert, jnp.sum(before * onehot, axis=1))


def local(tokens, grad_out, experts, gates, router_weight, saved_outputs):
    groups = lax.axis_size("expert")
    chosen_count = experts.shape[1]
    expert_count = router_weight.shape[0]
    held = expert_count // groups
    capacity = tokens.shape[0] // 2
    width = saved_outputs.shape[1]
    slot_expert, position = slot_positions(experts, expert_count)
    target = slot_expert % held * (groups * capacity) + slot_expert // held * capacity + position
    slot_gates = gates.reshape(-1)
    repeated = jnp.repeat(grad_out, chosen_count, axis=0)
    layout = (held, groups * capacity, width)
    returned = lax.all_to_all(
        saved_outputs.reshape(layout), "expert", split_axis=1, concat_axis=1, tiled=True
    )
    picked = returned.reshape(-1, width)[target]
    products = jnp.einsum("sd,sd->s", repeated, picked, preferred_element_type=jnp.float32)
    weighted = (slot_gates.astype(jnp.float32)[:, None] * repeated.astype(jnp.float32)).astype(
        jnp.bfloat16
    )
    buffer = jnp.zeros(saved_outputs.shape, jnp.bfloat16).at[target].set(weighted)
    expert_grad = lax.all_to_all(
        buffer.reshape(layout), "expert", split_axis=1, concat_axis=1, tiled=True
    ).reshape(-1, width)
    gate_grad = products.reshape(-1, chosen_count)
    gate_values = gates.astype(jnp.float32)
    blended = jnp.sum(gate_values * gate_grad, axis=1, keepdims=True)
    slot_grad = gate_values * (gate_grad - blended)
    onehot = (
        experts[:, :, None] == jnp.arange(expert_count, dtype=jnp.int32)[None, None, :]
    ).astype(jnp.float32)
    logit_grad = jnp.sum(onehot * slot_grad[:, :, None], axis=1).astype(jnp.bfloat16)
    partial_value = lax.dot_general(
        logit_grad, tokens, (((0,), (0,)), ((), ())), preferred_element_type=jnp.float32
    )
    summed = lax.psum(partial_value, ("dp", "expert"))
    scale_factor = float(lax.axis_size("dp") * groups * tokens.shape[0]) ** (-0.5)
    router_grad = summed * scale_factor
    input_grad = jnp.dot(logit_grad, router_weight, preferred_element_type=jnp.float32).astype(
        jnp.bfloat16
    )
    return (input_grad, router_grad, expert_grad)


def solution(mesh):
    return jax.shard_map(
        local,
        mesh=mesh,
        in_specs=(
            P(("dp", "expert"), None),
            P(("dp", "expert"), None),
            P(("dp", "expert"), None),
            P(("dp", "expert"), None),
            P(),
            P(("dp", "expert"), None),
        ),
        out_specs=(P(("dp", "expert"), None), P(), P(("dp", "expert"), None)),
        check_vma=False,
    )
```

profile of v0, /device:TPU:0, one launch (start us, length us, event | category | flops | bytes accessed | tf_op | source)
XLA Modules:
  0.0 228.8 jit_solution(14404547339752662202)
XLA Ops:
  7.2 0.0 copy-start
  7.2 8.7 %copy.40 = bf16[2,256,4096]{2,0,1:T(2,128)(2,1)} copy(bf16[2,256,4096]{2,1,0:T(8,128)(2,1)} %bitcast.20) | data formatting | bytes 8388608 | tf_op jit(solution)/shard_map/reshape | solution.py:27
  15.9 0.0 copy-start.4
  15.9 0.0 copy-start.1
  15.9 5.0 %all-to-all-start = ((bf16[2,256,4096]{2,0,1:T(2,128)(2,1)}), bf16[2,256,4096]{2,0,1:T(2,128)(2,1)}, u32[]{:S(2)}, u32[]{:S(2)}) async-start(bf16[2,256,4096]{2,0,1:T(2,128)(2,1)} %copy.40), calls=%async_computation | async-start | bytes 8388608 | tf_op jit(solution)/shard_map/all_to_all | solution.py:26
  20.9 0.0 copy-done.4
  20.9 0.0 copy-start.3
  20.9 0.1 copy.42
  21.0 0.1 eq.47
  21.2 0.1 eq.43
  21.3 0.1 reshape.177
  21.4 0.6 reduce-window.6
  22.0 0.2 slice_reduce_fusion
  22.3 0.0 copy-done.1
  22.3 3.5 %broadcast_in_dim.4 = bf16[128,2,4096]{2,1,0:T(2,128)(2,1)} broadcast(bf16[128,4096]{1,0:T(8,128)(2,1)S(1)} %copy-done.1), dimensions={0,2} | broadcast | bytes 3145728 | tf_op jit(solution)/shard_map/broadcast_in_dim | solution.py:24
  25.8 2.7 %reshape.179 = bf16[256,4096]{1,0:T(8,128)(2,1)S(1)} reshape(bf16[128,2,4096]{2,1,0:T(2,128)(2,1)} %broadcast_in_dim.4) | data formatting | bytes 4194304 | tf_op jit(solution)/shard_map/reshape | solution.py:24
  28.5 0.0 copy-done.3
  28.5 0.1 copy.47
  28.6 0.1 reshape.183
  28.8 0.1 fusion.7
  28.9 6.1 %scatter_custom_fusion = bf16[512,4096]{1,0:T(8,128)(2,1)} fusion(s32[256]{0:T(256)S(1)} %bitcast.22, bf16[256,4096]{1,0:T(8,128)(2,1)S(1)} %reshape.179, f32[256]{0:T(256)S(1)} %reshape.183, bf16[]{:T(256)} %constant.44.clone.1), kind=kCustom, calls=%fused_computation.7 | custom fusion | flops 3145728 | bytes 6292482 | tf_op jit(solution)/shard_map/scatter | solution.py:34
  35.0 8.6 %copy.48 = bf16[2,256,4096]{2,0,1:T(2,128)(2,1)} copy(bf16[2,256,4096]{2,1,0:T(8,128)(2,1)} %bitcast.19) | data formatting | bytes 8388608 | tf_op jit(solution)/shard_map/reshape | solution.py:36
  43.6 26.2 %all-to-all-done = bf16[2,256,4096]{2,0,1:T(2,128)(2,1)} async-done(((bf16[2,256,4096]{2,0,1:T(2,128)(2,1)}), bf16[2,256,4096]{2,0,1:T(2,128)(2,1)}, u32[]{:S(2)}, u32[]{:S(2)}) %all-to-all-start) | async-done | bytes 4194336 | tf_op jit(solution)/shard_map/all_to_all | solution.py:26
  69.8 4.9 %all-to-all-start.1 = ((bf16[2,256,4096]{2,0,1:T(2,128)(2,1)}), bf16[2,256,4096]{2,0,1:T(2,128)(2,1)}, u32[]{:S(2)}, u32[]{:S(2)}) async-start(bf16[2,256,4096]{2,0,1:T(2,128)(2,1)} %copy.48), calls=%async_computation.1 | async-start | bytes 8388608 | tf_op jit(solution)/shard_map/all_to_all | solution.py:35
  74.7 0.0 all-reduce.2.cloned.1.call-start
  74.8 7.1 %copy.41 = bf16[2,256,4096]{2,1,0:T(8,128)(2,1)} copy(bf16[2,256,4096]{2,0,1:T(2,128)(2,1)} %all-to-all-done) | data formatting | bytes 8388608 | tf_op jit(solution)/shard_map/all_to_all | solution.py:26
  81.9 8.0 %gather_fusion = bf16[256,4096]{1,0:T(8,128)(2,1)} fusion(bf16[512,4096]{1,0:T(8,128)(2,1)} %bitcast.18, s32[1024]{0:T(1024)S(1)} %pad_clamp_fusion), kind=kCustom, calls=%fused_computation | custom fusion | bytes 4195328 | tf_op jit(solution)/shard_map/gather | solution.py:29
  89.8 0.0 copy-start.2
  89.8 2.2 fusion
  92.1 0.1 reshape.180
  92.2 0.1 copy.46
  92.4 0.0 copy-done
  92.4 0.9 fusion.15
  93.3 0.0 all-reduce.2.cloned.1.call-update
  93.3 0.0 copy-done.2
  93.3 1.4 convolution_convert_fusion
  94.8 28.4 %all-to-all-done.1 = bf16[2,256,4096]{2,0,1:T(2,128)(2,1)} async-done(((bf16[2,256,4096]{2,0,1:T(2,128)(2,1)}), bf16[2,256,4096]{2,0,1:T(2,128)(2,1)}, u32[]{:S(2)}, u32[]{:S(2)}) %all-to-all-start.1) | async-done | bytes 4194336 | tf_op jit(solution)/shard_map/all_to_all | solution.py:35
  123.2 7.1 %copy.49 = bf16[2,256,4096]{2,1,0:T(8,128)(2,1)} copy(bf16[2,256,4096]{2,0,1:T(2,128)(2,1)} %all-to-all-done.1) | data formatting | bytes 8388608 | tf_op jit(solution)/shard_map/all_to_all | solution.py:35
  130.3 90.1 %all-reduce.2.cloned.1.call-done = f32[8,4096]{1,0:T(8,128)} async-done(((f32[8,4096]{1,0:T(8,128)}), f32[8,4096]{1,0:T(8,128)}) %all-reduce.2.cloned.1.call-update) | async-done | bytes 131088 | tf_op jit(solution)/shard_map/psum | solution.py:49
  220.4 1.6 broadcast_multiply_fusion
  (8 shorter events, 0.1 us)
Async XLA Ops:
  7.2 85.2 %copy-start = (bf16[128,4096]{1,0:T(8,128)(2,1)S(1)}, bf16[128,4096]{1,0:T(8,128)(2,1)}, u32[]{:S(2)}) copy-start(bf16[128,4096]{1,0:T(8,128)(2,1)} %param.6) | copy-start | bytes 3145732
  15.9 5.0 %copy-start.4 = (s32[128,2]{0,1:T(2,128)S(1)}, s32[128,2]{0,1:T(2,128)}, u32[]{:S(2)}) copy-start(s32[128,2]{0,1:T(2,128)} %param.8) | copy-start | bytes 3076
  15.9 6.4 %copy-start.1 = (bf16[128,4096]{1,0:T(8,128)(2,1)S(1)}, bf16[128,4096]{1,0:T(8,128)(2,1)}, u32[]{:S(2)}) copy-start(bf16[128,4096]{1,0:T(8,128)(2,1)} %param.7) | copy-start | bytes 3145732
  15.9 53.9 %all-to-all-start = ((bf16[2,256,4096]{2,0,1:T(2,128)(2,1)}), bf16[2,256,4096]{2,0,1:T(2,128)(2,1)}, u32[]{:S(2)}, u32[]{:S(2)}) async-start(bf16[2,256,4096]{2,0,1:T(2,128)(2,1)} %copy.40), calls=%async_computation | async-start | bytes 8388608 | tf_op jit(solution)/shard_map/all_to_all | solution.py:26
  20.9 7.6 %copy-start.3 = (bf16[128,2]{0,1:T(2,128)(2,1)S(1)}, bf16[128,2]{0,1:T(2,128)(2,1)}, u32[]{:S(2)}) copy-start(bf16[128,2]{0,1:T(2,128)(2,1)} %param.9) | copy-start | bytes 1540
  69.8 53.4 %all-to-all-start.1 = ((bf16[2,256,4096]{2,0,1:T(2,128)(2,1)}), bf16[2,256,4096]{2,0,1:T(2,128)(2,1)}, u32[]{:S(2)}, u32[]{:S(2)}) async-start(bf16[2,256,4096]{2,0,1:T(2,128)(2,1)} %copy.48), calls=%async_computation.1 | async-start | bytes 8388608 | tf_op jit(solution)/shard_map/all_to_all | solution.py:35
  74.7 145.7 %all-reduce.2.cloned.1.call-start = ((), (), s32[]{:S(2)}) async-start(), calls=%async_computation.2 | async-start | bytes 262144 | tf_op jit(solution)/shard_map/psum | solution.py:49
  89.8 3.5 %copy-start.2 = (bf16[8,4096]{1,0:T(8,128)(2,1)S(1)}, bf16[8,4096]{1,0:T(8,128)(2,1)}, u32[]{:S(2)}) copy-start(bf16[8,4096]{1,0:T(8,128)(2,1)} %param.10) | copy-start | bytes 196612
Sparse Core Ops, SparseCore 0:
  93.4 126.8 all-reduce.1
where the time goes:
time: 229 us
  waiting for transfers between devices  145 us (63%)
  local copies, waits for them, and re-layouts  46.9 us (20%)
  between operations  14.2 us (6%)
  other arithmetic  10.7 us (5%)
  starting transfers between devices  9.97 us (4%)
  matrix products  2.36 us (1%)
    psum x1, waiting for transfers between devices, local(): summed = lax.psum(partial_value, ('dp', 'expert'))  90.1 us
    all_to_all x1, waiting for transfers between devices, local(): lax.all_to_all(buffer.reshape(layout), 'expert', split_axis=1, concat_axi...  28.4 us
    all_to_all x1, waiting for transfers between devices, local(): lax.all_to_all(saved_outputs.reshape(layout), 'expert', split_axis=1, con...  26.2 us
    reshape x1, local copies, waits for them, and re-layouts, local(): saved_outputs.reshape(layout)  8.69 us
    reshape x1, local copies, waits for them, and re-layouts, local(): buffer.reshape(layout)  8.56 us
    gather x1, local copies, waits for them, and re-layouts, local(): picked = returned.reshape(-1, width)[target]  7.96 us
    all_to_all x1, local copies, waits for them, and re-layouts, local(): lax.all_to_all(buffer.reshape(layout), 'expert', split_axis=1, concat_axi...  7.13 us
    all_to_all x1, local copies, waits for them, and re-layouts, local(): lax.all_to_all(saved_outputs.reshape(layout), 'expert', split_axis=1, con...  7.11 us
  transfers between devices with their start and end apart: 3, of which 3 were waited for; matrix products, arithmetic and copies ran while one was open for 22% of the time, Pallas kernels for 0%

commit v1 on v0

--- a/solution.py
+++ b/solution.py
@@ -46,7 +46,8 @@
     partial_value = lax.dot_general(
         logit_grad, tokens, (((0,), (0,)), ((), ())), preferred_element_type=jnp.float32
     )
-    summed = lax.psum(partial_value, ("dp", "expert"))
+    row_out = lax.all_gather(partial_value, ("dp", "expert"))
+    summed = jnp.sum(row_out, axis=0)
     scale_factor = float(lax.axis_size("dp") * groups * tokens.shape[0]) ** (-0.5)
     router_grad = summed * scale_factor
     input_grad = jnp.dot(logit_grad, router_weight, preferred_element_type=jnp.float32).astype(

time: 229 us -> 178 us (0.78)
  waiting for transfers between devices: 145 us -> 40.9 us
  blocking collectives: 0 us -> 60 us
  starting transfers between devices: 9.97 us -> 5.21 us
  local copies, waits for them, and re-layouts: 46.9 us -> 42.7 us
    psum x1 -> x0, waiting for transfers between devices: 90.1 us -> none  [local(): summed = lax.psum(partial_value, ('dp', 'expert'))]
    all_to_all x0 -> x1, blocking collectives: none -> 60 us  [local(): lax.all_to_all(buffer.reshape(layout), 'expert', split_axis=1, concat_axi...]
    all_to_all x1 -> x0, waiting for transfers between devices: 28.4 us -> none  [local(): lax.all_to_all(buffer.reshape(layout), 'expert', split_axis=1, concat_axi...]
    all_to_all x1, waiting for transfers between devices: 26.2 us -> 40.9 us  [local(): lax.all_to_all(saved_outputs.reshape(layout), 'expert', split_axis=1, con...]
    all_to_all x1 -> x0, starting transfers between devices: 4.94 us -> none  [local(): lax.all_to_all(buffer.reshape(layout), 'expert', split_axis=1, concat_axi...]
    reduce_sum x0 -> x1, other arithmetic: none -> 2.4 us  [local(): summed = jnp.sum(row_out, axis=0)]
  transfers between devices with their start and end apart: 3 -> 2, of which waited for: 3 -> 1; matrix products, arithmetic and copies ran while one was open for 22% -> 15% of each run, Pallas kernels for 0% -> 0%
where the time goes in v1:
time: 178 us
  blocking collectives  60 us (34%)
  local copies, waits for them, and re-layouts  42.7 us (24%)
  waiting for transfers between devices  40.9 us (23%)
  between operations  14.1 us (8%)
  other arithmetic  12.5 us (7%)
  starting transfers between devices  5.21 us (3%)
  matrix products  2.36 us (1%)
    all_to_all x1, blocking collectives, local(): lax.all_to_all(buffer.reshape(layout), 'expert', split_axis=1, concat_axi...  60 us
    all_to_all x1, waiting for transfers between devices, local(): lax.all_to_all(saved_outputs.reshape(layout), 'expert', split_axis=1, con...  40.9 us
    reshape x1, local copies, waits for them, and re-layouts, local(): saved_outputs.reshape(layout)  8.69 us
    gather x1, local copies, waits for them, and re-layouts, local(): picked = returned.reshape(-1, width)[target]  7.96 us
    all_to_all x1, local copies, waits for them, and re-layouts, local(): lax.all_to_all(saved_outputs.reshape(layout), 'expert', split_axis=1, con...  7.11 us
    reshape x1, local copies, waits for them, and re-layouts, local(): buffer.reshape(layout)  6.59 us
    scatter x1, other arithmetic, local(): jnp.zeros(saved_outputs.shape, jnp.bfloat16).at[target].set(weighted)  6.36 us
    all_to_all x1, starting transfers between devices, local(): lax.all_to_all(saved_outputs.reshape(layout), 'expert', split_axis=1, con...  4.99 us
  transfers between devices with their start and end apart: 2, of which 1 were waited for; matrix products, arithmetic and copies ran while one was open for 15% of the time, Pallas kernels for 0%

profile of v1, /device:TPU:0, one launch (start us, length us, event | category | flops | bytes accessed | tf_op | source)
XLA Modules:
  0.0 177.7 jit_solution(8461542470771208002)
XLA Ops:
  7.2 0.0 copy-start
  7.2 8.7 %copy.40 = bf16[2,256,4096]{2,0,1:T(2,128)(2,1)} copy(bf16[2,256,4096]{2,1,0:T(8,128)(2,1)} %bitcast.22) | data formatting | bytes 8388608 | tf_op jit(solution)/shard_map/reshape | solution.py:27
  15.9 0.0 copy-start.4
  15.9 0.0 copy-start.1
  15.9 5.0 %all-to-all-start = ((bf16[2,256,4096]{2,0,1:T(2,128)(2,1)}), bf16[2,256,4096]{2,0,1:T(2,128)(2,1)}, u32[]{:S(2)}, u32[]{:S(2)}) async-start(bf16[2,256,4096]{2,0,1:T(2,128)(2,1)} %copy.40), calls=%async_computation | async-start | bytes 8388608 | tf_op jit(solution)/shard_map/all_to_all | solution.py:26
  20.9 0.2 all-gather.3.cloned.1.call-start
  21.1 0.0 copy-done.4
  21.1 0.1 copy.42
  21.2 0.1 eq.47
  21.4 0.1 eq.43
  21.5 0.1 reshape.177
  21.7 0.6 reduce-window.6
  22.3 0.2 slice_reduce_fusion
  22.5 0.0 copy-done.1
  22.5 3.5 %broadcast_in_dim.4 = bf16[128,2,4096]{2,1,0:T(2,128)(2,1)} broadcast(bf16[128,4096]{1,0:T(8,128)(2,1)S(1)} %copy-done.1), dimensions={0,2} | broadcast | bytes 3145728 | tf_op jit(solution)/shard_map/broadcast_in_dim | solution.py:24
  26.0 2.7 %reshape.179 = bf16[256,4096]{1,0:T(8,128)(2,1)S(1)} reshape(bf16[128,2,4096]{2,1,0:T(2,128)(2,1)} %broadcast_in_dim.4) | data formatting | bytes 4194304 | tf_op jit(solution)/shard_map/reshape | solution.py:24
  28.7 0.1 fusion.7
  28.8 40.9 %all-to-all-done = bf16[2,256,4096]{2,0,1:T(2,128)(2,1)} async-done(((bf16[2,256,4096]{2,0,1:T(2,128)(2,1)}), bf16[2,256,4096]{2,0,1:T(2,128)(2,1)}, u32[]{:S(2)}, u32[]{:S(2)}) %all-to-all-start) | async-done | bytes 4194336 | tf_op jit(solution)/shard_map/all_to_all | solution.py:26
  69.8 7.1 %copy.41 = bf16[2,256,4096]{2,1,0:T(8,128)(2,1)} copy(bf16[2,256,4096]{2,0,1:T(2,128)(2,1)} %all-to-all-done) | data formatting | bytes 8388608 | tf_op jit(solution)/shard_map/all_to_all | solution.py:26
  76.9 8.0 %gather_fusion = bf16[256,4096]{1,0:T(8,128)(2,1)} fusion(bf16[512,4096]{1,0:T(8,128)(2,1)} %bitcast.20, s32[1024]{0:T(1024)S(1)} %pad_clamp_fusion), kind=kCustom, calls=%fused_computation | custom fusion | bytes 4195328 | tf_op jit(solution)/shard_map/gather | solution.py:29
  84.8 0.0 copy-start.3
  84.8 2.2 %fusion = f32[256]{0:T(256)S(1)} fusion(bf16[256,4096]{1,0:T(8,128)(2,1)S(1)} %reshape.179, bf16[256,4096]{1,0:T(8,128)(2,1)} %gather_fusion), kind=kLoop, calls=%fused_computation.5 | loop fusion | flops 4194048 | bytes 4195328 | tf_op jit(solution)/shard_map/sd,sd->s/dot_general | solution.py:30
  87.1 0.1 reshape.180
  87.2 0.1 copy.46
  87.3 0.0 copy-done.3
  87.3 0.0 copy-done
  87.3 0.9 fusion.15
  88.3 0.0 all-gather.3.cloned.1.call-update
  88.3 0.1 copy.47
  88.4 0.1 reshape.183
  88.5 6.4 %scatter_custom_fusion = bf16[512,4096]{1,0:T(8,128)(2,1)} fusion(s32[256]{0:T(256)S(1)} %bitcast.25, bf16[256,4096]{1,0:T(8,128)(2,1)S(1)} %reshape.179, f32[256]{0:T(256)S(1)} %reshape.183, bf16[]{:T(256)} %constant.44.clone.1), kind=kCustom, calls=%fused_computation.8 | custom fusion | flops 3145728 | bytes 6292482 | tf_op jit(solution)/shard_map/scatter | solution.py:34
  94.9 6.6 %copy.48 = bf16[2,256,4096]{2,0,1:T(2,128)(2,1)S(1)} copy(bf16[2,256,4096]{2,1,0:T(8,128)(2,1)} %bitcast.21) | data formatting | bytes 8388608 | tf_op jit(solution)/shard_map/reshape | solution.py:36
  101.5 60.0 %all_to_all.10 = bf16[2,256,4096]{2,0,1:T(2,128)(2,1)S(1)} all-to-all(bf16[2,256,4096]{2,0,1:T(2,128)(2,1)S(1)} %copy.48), channel_id=1, replica_groups=mesh['dp'=8,'expert'=4] {'expert'}, dimensions={1} | all-to-all | bytes 8388608 | tf_op jit(solution)/shard_map/all_to_all | solution.py:35
  161.5 0.0 copy-start.2
  161.5 4.9 %copy.49 = bf16[2,256,4096]{2,1,0:T(8,128)(2,1)} copy(bf16[2,256,4096]{2,0,1:T(2,128)(2,1)S(1)} %all_to_all.10) | data formatting | bytes 8388608 | tf_op jit(solution)/shard_map/all_to_all | solution.py:35
  166.4 0.0 copy-done.2
  166.4 1.4 convolution_convert_fusion
  167.8 0.0 all-gather.3.cloned.1.call-done
  167.8 2.4 %bitcast_reduce_fusion = f32[8,4096]{1,0:T(8,128)S(1)} fusion(f32[256,4096]{1,0:T(8,128)} %all-gather.3.cloned.1.call-done), kind=kLoop, calls=%fused_computation.7 | loop fusion | flops 1015808 | bytes 4325376 | tf_op jit(solution)/shard_map/reduce_sum | solution.py:50
  170.2 0.7 broadcast_multiply_fusion
  (8 shorter events, 0.1 us)
Async XLA Ops:
  7.2 80.2 %copy-start = (bf16[128,4096]{1,0:T(8,128)(2,1)S(1)}, bf16[128,4096]{1,0:T(8,128)(2,1)}, u32[]{:S(2)}) copy-start(bf16[128,4096]{1,0:T(8,128)(2,1)} %param.6) | copy-start | bytes 3145732
  15.9 5.2 %copy-start.4 = (s32[128,2]{0,1:T(2,128)S(1)}, s32[128,2]{0,1:T(2,128)}, u32[]{:S(2)}) copy-start(s32[128,2]{0,1:T(2,128)} %param.8) | copy-start | bytes 3076
  15.9 6.6 %copy-start.1 = (bf16[128,4096]{1,0:T(8,128)(2,1)S(1)}, bf16[128,4096]{1,0:T(8,128)(2,1)}, u32[]{:S(2)}) copy-start(bf16[128,4096]{1,0:T(8,128)(2,1)} %param.7) | copy-start | bytes 3145732
  15.9 53.9 %all-to-all-start = ((bf16[2,256,4096]{2,0,1:T(2,128)(2,1)}), bf16[2,256,4096]{2,0,1:T(2,128)(2,1)}, u32[]{:S(2)}, u32[]{:S(2)}) async-start(bf16[2,256,4096]{2,0,1:T(2,128)(2,1)} %copy.40), calls=%async_computation | async-start | bytes 8388608 | tf_op jit(solution)/shard_map/all_to_all | solution.py:26
  20.9 146.9 %all-gather.3.cloned.1.call-start = ((), (), s32[]{:S(2)}) async-start(), calls=%async_computation.2 | async-start | bytes 4325376 | tf_op jit(solution)/shard_map/all_gather | solution.py:49
  84.8 2.4 %copy-start.3 = (bf16[128,2]{0,1:T(2,128)(2,1)S(1)}, bf16[128,2]{0,1:T(2,128)(2,1)}, u32[]{:S(2)}) copy-start(bf16[128,2]{0,1:T(2,128)(2,1)} %param.9) | copy-start | bytes 1540
  161.5 4.9 %copy-start.2 = (bf16[8,4096]{1,0:T(8,128)(2,1)S(1)}, bf16[8,4096]{1,0:T(8,128)(2,1)}, u32[]{:S(2)}) copy-start(bf16[8,4096]{1,0:T(8,128)(2,1)} %param.10) | copy-start | bytes 196612
Sparse Core Ops, SparseCore 0:
  88.4 70.3 all-gather.2
